TPU v7x, 32 devices: a whole 2x2x4 slice. The times are simulated.
32 devices in a mesh: groups: 2 (over x), space: 16 (over z, y, core).
Axes of the slice: x: 2, y: 2, z: 4, core: 2. Of those that a mesh axis runs over, the one named last changes fastest.
Arguments:
- inputs: bfloat16 [768, 1152, 256], P(('groups', 'space')), parts along dimension 0, may hold values from -6 to 6
- spectral_weight: bfloat16 [2, 256, 2, 256, 256], P(None, 'space'), may hold values from -0.25 to 0.25
- local_weight: bfloat16 [2, 256, 256], replicated, may hold values from -0.375 to 0.375
- layer_bias: bfloat16 [2, 256], replicated, may hold values from -3 to 3
- readout_hidden: bfloat16 [256, 256], replicated, may hold values from -0.375 to 0.375
- readout_final: bfloat16 [20, 256], replicated, may hold values from -0.375 to 0.375
Outputs:
- forecast: bfloat16 [20, 768, 1152], P(None, ('groups', 'space')), parts along dimension 1
There are 2 independent parts, one for each index of `groups`. A program takes and returns all parts, laid end to end along the dimension named above; an argument that names none is the same for every part. Nothing has to cross between parts.
All inputs are finite; a program needn't handle non-finite values.
Results may differ from a plain program's by a relative error of at most 0.018.
Values may be sent and summed in bfloat16 or wider, within the bound.
A program may use at most 128 MiB of HBM per device.

v0:
```python
import jax
import jax.numpy as jnp
from jax import lax
from jax.sharding import PartitionSpec as P

KY = 16
KX = 16
LAYERS = 2
MODES = 256


def zonal_tables(columns, modes):
    column_ids = jnp.arange(columns, dtype=jnp.int32)
    wave_numbers = jnp.arange(1, modes + 1, dtype=jnp.int32)
    phase_int = column_ids[:, None] * wave_numbers[None, :] % columns
    angles = 2.0 * jnp.pi / columns * phase_int.astype(jnp.float32)
    cosines = jnp.cos(angles)
    sines = jnp.sin(angles)
    forward = jnp.concatenate([cosines, -sines], axis=1) / jnp.sqrt(jnp.float32(columns))
    inverse = jnp.stack([cosines, -sines], axis=2).reshape(columns, 2 * modes) * jnp.sqrt(
        jnp.float32(2.0 / modes)
    )
    return (forward.astype(jnp.bfloat16), inverse.astype(jnp.bfloat16))


def meridional_tables(row_ids, height, modes):
    mode_index = jnp.arange(modes, dtype=jnp.int32)
    wave_numbers = jnp.where(mode_index < modes // 2, mode_index, mode_index - modes)
    phase_int = wave_numbers[:, None] * row_ids[None, :] % height
    angles = 2.0 * jnp.pi / height * phase_int.astype(jnp.float32)
    cosines = jnp.cos(angles)
    sines = jnp.sin(angles)
    forward = jnp.stack(
        [jnp.stack([cosines, sines], axis=2), jnp.stack([-sines, cosines], axis=2)], axis=1
    )
    forward = forward / jnp.sqrt(jnp.float32(height))
    cos_rows = cosines.T
    sin_rows = sines.T
    inverse = jnp.stack(
        [jnp.stack([cos_rows, -sin_rows], axis=2), jnp.stack([sin_rows, cos_rows], axis=2)], axis=1
    )
    inverse = inverse / jnp.sqrt(jnp.float32(modes))
    return (forward.astype(jnp.bfloat16), inverse.astype(jnp.bfloat16))


def mix_modes(spectrum, weights):
    real_in = spectrum[:, 0]
    imag_in = spectrum[:, 1]
    real_weight = weights[:, 0]
    imag_weight = weights[:, 1]

    def product(vectors, matrices):
        return jnp.einsum("mi,mio->mo", vectors, matrices, preferred_element_type=jnp.float32)

    real_out = product(real_in, real_weight) - product(imag_in, imag_weight)
    imag_out = product(real_in, imag_weight) + product(imag_in, real_weight)
    return jnp.stack([real_out, imag_out], axis=1).astype(jnp.bfloat16)


def per_device(inputs, spectral_weight, local_weight, layer_bias, readout_hidden, readout_final):
    rows_here, columns, channels = inputs.shape
    devices_along = lax.axis_size("space")
    height = rows_here * devices_along
    zonal_forward, zonal_inverse = zonal_tables(columns, KX)
    local_rows = jnp.arange(rows_here, dtype=jnp.int32) * devices_along + lax.axis_index("space")
    forward_here, inverse_here = meridional_tables(local_rows, height, KY)
    current = inputs
    for layer_index in range(LAYERS):
        zonal_part = jnp.einsum(
            "hwc,wj->hjc", current, zonal_forward, preferred_element_type=jnp.float32
        )
        zonal_view = zonal_part.astype(jnp.bfloat16).reshape(rows_here, 2, KX, channels)
        partial_value = jnp.einsum(
            "qphr,hrkc->qkpc", forward_here, zonal_view, preferred_element_type=jnp.float32
        )
        partial_value = partial_value.reshape(MODES, 2 * channels)
        spectrum = lax.psum_scatter(
            partial_value, "space", scatter_dimension=0, tiled=True
        ).reshape(-1, 2, channels)
        mixed = mix_modes(spectrum.astype(jnp.bfloat16), spectral_weight[layer_index])
        all_modes = lax.all_gather(mixed, "space", axis=0, tiled=True).reshape(KY, KX, 2, channels)
        returned = jnp.einsum(
            "hpqr,qkrc->hkpc", inverse_here, all_modes, preferred_element_type=jnp.float32
        )
        returned = returned.astype(jnp.bfloat16).reshape(rows_here, 2 * KX, channels)
        spread = jnp.einsum(
            "wj,hjc->hwc", zonal_inverse, returned, preferred_element_type=jnp.float32
        )
        pointwise = jnp.dot(
            current.reshape(-1, channels),
            local_weight[layer_index],
            preferred_element_type=jnp.float32,
        )
        pointwise = pointwise.reshape(current.shape)
        bias_now = layer_bias[layer_index].astype(jnp.float32)
        current = jax.nn.gelu(spread + pointwise + bias_now, approximate=True).astype(jnp.bfloat16)
    hidden = jnp.dot(
        current.reshape(-1, channels), readout_hidden, preferred_element_type=jnp.float32
    )
    hidden = jax.nn.gelu(hidden, approximate=True).astype(jnp.bfloat16)
    final = jnp.einsum("pq,nq->pn", readout_final, hidden, preferred_element_type=jnp.float32)
    return final.astype(jnp.bfloat16).reshape(readout_final.shape[0], rows_here, columns)


def solution(mesh):
    in_specs = (
        P(("groups", "space"), None, None),
        P(None, "space", None, None, None),
        P(),
        P(),
        P(),
        P(),
    )
    out_specs = P(None, ("groups", "space"), None)
    return jax.shard_map(
        per_device, mesh=mesh, in_specs=in_specs, out_specs=out_specs, check_vma=False
    )
```

profile of v0, /device:TPU:0, one launch (start us, length us, event | category | flops | bytes accessed | tf_op | source)
XLA Modules:
  0.0 308.6 jit_solution(3359486465415475526)
XLA Ops:
  6.5 0.0 copy-start
  6.5 0.0 copy-start.1
  6.5 0.0 reduce-scatter.3.cloned.1.call-start
  6.6 0.4 fusion.64
  7.0 0.1 fusion.101
  7.1 7.5 %convolution_convert_fusion.2 = bf16[32,24,256]{2,0,1:T(8,128)(2,1)S(1)} fusion(bf16[24,1152,256]{2,1,0:T(8,128)(2,1)} %param.6, f32[1152,16]{0,1:T(8,128)S(1)} %get-tuple-element.26, f32[1152,16]{0,1:T(8,128)S(1)} %get-tuple-element.25), kind=kOutput, calls=%fused_computation.49 | convolution fusion | flops 453292032 | bytes 14696448 | tf_op jit(solution)/shard_map/hwc,wj->hjc/dot_general | solution.py:69
  14.6 0.4 convolution_bitcast_fusion.3
  15.0 0.4 copy.42
  15.4 0.8 copy.96
  16.3 0.0 reduce-scatter.3.cloned.1.call-update
  16.3 0.0 reduce-scatter.5.cloned.1.call-start
  16.3 0.1 fusion.110
  16.5 0.4 fusion.61
  16.9 0.0 copy-done.1
  16.9 6.0 %slice_bitcast_fusion.1 = (bf16[16,2,256,256]{3,2,1,0:T(8,128)(2,1)}, bf16[16,2,256,256]{3,2,1,0:T(8,128)(2,1)}) fusion(bf16[2,16,2,256,256]{4,3,2,1,0:T(8,128)(2,1)} %param.7), kind=kLoop, calls=%fused_computation.33 | loop fusion | bytes 16777216 | tf_op jit(solution)/shard_map/squeeze | solution.py:80
  22.8 52.5 %reduce-scatter.3.cloned.1.call-done = f32[16,512]{1,0:T(8,128)} async-done(((f32[256,512]{1,0:T(8,128)}), f32[16,512]{1,0:T(8,128)}) %reduce-scatter.3.cloned.1.call-update) | async-done | bytes 32784 | tf_op jit(solution)/shard_map/reduce_scatter | solution.py:77
  75.3 0.8 convert_element_type.150
  76.1 2.0 fusion.29
  78.1 2.0 fusion.28
  80.1 2.0 fusion.27
  82.1 2.0 fusion.30
  84.1 20.3 %all_gather.6 = bf16[256,2,256]{2,0,1:T(8,128)(2,1)S(1)} all-gather(bf16[16,2,256]{2,0,1:T(8,128)(2,1)S(1)} %pad_maximum_fusion), channel_id=1, replica_groups=mesh['groups'=2,'space'=16] {'space'}, dimensions={0}, use_global_device_ids=true | all-gather | bytes 278528 | tf_op jit(solution)/shard_map/all_gather | solution.py:81
  104.4 0.3 fusion.38
  104.7 0.0 copy-start.2
  104.7 11.4 %fusion.43 = f32[24,256,1152,1]{2,1,3,0:T(8,128)} fusion(bf16[24,16,2,256]{3,0,2,1:T(8,128)(2,1)S(1)} %fusion.38, f32[1152,16,1]{0,1,2:T(8,128)S(1)} %get-tuple-element.24, f32[1152,16,1]{0,1,2:T(8,128)S(1)} %get-tuple-element.23), kind=kOutput, calls=%fused_computation.60 | convolution fusion | flops 453095424 | bytes 28852224 | tf_op jit(solution)/shard_map/wj,hjc->hwc/dot_general | solution.py:86
  116.1 0.0 copy-done.2
  116.1 24.0 %fusion.7 = bf16[24,1152,256]{1,2,0:T(8,128)(2,1)} fusion(f32[24,256,1152,1]{2,1,3,0:T(8,128)} %fusion.43, bf16[24,1152,256]{2,1,0:T(8,128)(2,1)} %param.6, f32[256]{0:T(256)S(1)} %bitcast.212, bf16[2,256,256]{2,1,0:T(8,128)(2,1)S(1)} %copy-done.2), kind=kOutput, calls=%fused_computation.11 | convolution fusion | flops 3701735424 | bytes 56755200 | tf_op jit(solution)/shard_map/dot_general | solution.py:89
  140.1 9.3 %convolution_convert_fusion.1 = bf16[32,24,256]{2,0,1:T(8,128)(2,1)S(1)} fusion(bf16[24,1152,256]{1,2,0:T(8,128)(2,1)} %fusion.7, f32[1152,16]{0,1:T(8,128)S(1)} %get-tuple-element.26, f32[1152,16]{0,1:T(8,128)S(1)} %get-tuple-element.25), kind=kOutput, calls=%fused_computation.48 | convolution fusion | flops 453292032 | bytes 14696448 | tf_op jit(solution)/shard_map/hwc,wj->hjc/dot_general | solution.py:69
  149.4 0.3 convolution_bitcast_fusion.2
  149.8 0.4 copy.50
  150.2 0.8 copy.97
  151.0 0.0 reduce-scatter.5.cloned.1.call-update
  151.0 53.6 %reduce-scatter.5.cloned.1.call-done = f32[16,512]{1,0:T(8,128)} async-done(((f32[256,512]{1,0:T(8,128)}), f32[16,512]{1,0:T(8,128)}) %reduce-scatter.5.cloned.1.call-update) | async-done | bytes 32784 | tf_op jit(solution)/shard_map/reduce_scatter | solution.py:77
  204.6 0.8 convert_element_type.163
  205.4 2.0 fusion.31
  207.4 2.0 fusion.34
  209.4 2.0 fusion.33
  211.3 2.0 fusion.32
  213.4 20.3 %all_gather.7 = bf16[256,2,256]{2,0,1:T(8,128)(2,1)S(1)} all-gather(bf16[16,2,256]{2,0,1:T(8,128)(2,1)S(1)} %pad_maximum_fusion.1), channel_id=1, replica_groups=mesh['groups'=2,'space'=16] {'space'}, dimensions={0}, use_global_device_ids=true | all-gather | bytes 278528 | tf_op jit(solution)/shard_map/all_gather | solution.py:81
  233.7 0.3 fusion.37
  234.0 11.4 %fusion.41 = f32[24,256,1152,1]{2,1,3,0:T(8,128)} fusion(bf16[24,16,2,256]{3,0,2,1:T(8,128)(2,1)S(1)} %fusion.37, f32[1152,16,1]{0,1,2:T(8,128)S(1)} %get-tuple-element.24, f32[1152,16,1]{0,1,2:T(8,128)S(1)} %get-tuple-element.23), kind=kOutput, calls=%fused_computation.58 | convolution fusion | flops 453095424 | bytes 28852224 | tf_op jit(solution)/shard_map/wj,hjc->hwc/dot_general | solution.py:86
  245.4 24.4 %fusion.15 = bf16[24,1152,256]{1,2,0:T(8,128)(2,1)} fusion(f32[24,256,1152,1]{2,1,3,0:T(8,128)} %fusion.41, bf16[24,1152,256]{1,2,0:T(8,128)(2,1)} %fusion.7, f32[256]{0:T(256)S(1)} %bitcast.211, bf16[2,256,256]{2,1,0:T(8,128)(2,1)S(1)} %copy-done.2), kind=kOutput, calls=%fused_computation.19 | convolution fusion | flops 3701735424 | bytes 56755200 | tf_op jit(solution)/shard_map/dot_general | solution.py:89
  269.8 0.0 copy-start.3
  269.8 18.7 %copy.57 = bf16[24,1152,256]{2,1,0:T(8,128)(2,1)} copy(bf16[24,1152,256]{1,2,0:T(8,128)(2,1)} %fusion.15) | data formatting | bytes 28311552 | tf_op jit(solution)/shard_map/convert_element_type | solution.py:96
  288.5 0.0 copy-done
  288.5 0.0 copy-done.3
  288.5 12.0 %convolution_convert_fusion = bf16[27648,20]{0,1:T(8,128)(2,1)S(1)} fusion(bf16[20,256]{1,0:T(8,128)(2,1)S(1)} %copy-done.3, bf16[27648,256]{1,0:T(8,128)(2,1)} %bitcast.196, bf16[256,256]{1,0:T(8,128)(2,1)S(1)} %copy-done), kind=kOutput, calls=%fused_computation.3 | convolution fusion | flops 3971248128 | bytes 15403008 | tf_op jit(solution)/shard_map/pq,nq->pn/dot_general | solution.py:101
  300.5 0.2 copy.98
  300.6 1.1 slice.64
  (19 shorter events, 0.2 us)
Async XLA Ops:
  6.5 282.0 %copy-start = (bf16[256,256]{1,0:T(8,128)(2,1)S(1)}, bf16[256,256]{1,0:T(8,128)(2,1)}, u32[]{:S(2)}) copy-start(bf16[256,256]{1,0:T(8,128)(2,1)} %param.10) | copy-start | bytes 393220
  6.5 10.3 %copy-start.1 = (bf16[2,256]{1,0:T(2,128)(2,1)S(1)}, bf16[2,256]{1,0:T(2,128)(2,1)}, u32[]{:S(2)}) copy-start(bf16[2,256]{1,0:T(2,128)(2,1)} %param.9) | copy-start | bytes 3076
  6.5 68.8 %reduce-scatter.3.cloned.1.call-start = ((), (), s32[]{:S(2)}) async-start(), calls=%async_computation.2 | async-start | bytes 557056 | tf_op jit(solution)/shard_map/reduce_scatter | solution.py:77
  16.3 188.3 %reduce-scatter.5.cloned.1.call-start = ((), (), s32[]{:S(2)}) async-start(), calls=%async_computation.3 | async-start | bytes 557056 | tf_op jit(solution)/shard_map/reduce_scatter | solution.py:77
  104.7 11.4 %copy-start.2 = (bf16[2,256,256]{2,1,0:T(8,128)(2,1)S(1)}, bf16[2,256,256]{2,1,0:T(8,128)(2,1)}, u32[]{:S(2)}) copy-start(bf16[2,256,256]{2,1,0:T(8,128)(2,1)} %param.8) | copy-start | bytes 786436
  269.8 18.7 %copy-start.3 = (bf16[20,256]{1,0:T(8,128)(2,1)S(1)}, bf16[20,256]{1,0:T(8,128)(2,1)}, u32[]{:S(2)}) copy-start(bf16[20,256]{1,0:T(8,128)(2,1)} %param.11) | copy-start | bytes 30724
Sparse Core Ops, SparseCore 0:
  16.4 58.8 reduce-scatter.2
  151.1 53.3 reduce-scatter.4
where the time goes:
time: 310 us; the launch traced here: 309 us
  matrix products  117 us (38%)
  waiting for transfers between devices  106 us (34%)
  blocking collectives  40.7 us (13%)
  local copies, waits for them, and re-layouts  28.5 us (9%)
  between operations  13.6 us (4%)
    reduce_scatter x2, waiting for transfers between devices, per_device(): lax.psum_scatter(partial_value, 'space', scatter_dimension=0, tiled=True)  106 us
    dot_general x2, matrix products, per_device(): jnp.dot(current.reshape(-1, channels), local_weight[layer_index], preferr...  48.4 us
    all_gather x2, blocking collectives, per_device(): lax.all_gather(mixed, 'space', axis=0, tiled=True)  40.7 us
    dot_general x2, matrix products, per_device(): jnp.einsum('wj,hjc->hwc', zonal_inverse, returned, preferred_element_type...  22.8 us
    convert_element_type x1, local copies, waits for them, and re-layouts, per_device(): jax.nn.gelu(spread + pointwise + bias_now, approximate=True)  18.7 us
    dot_general x2, matrix products, per_device(): jnp.einsum('hwc,wj->hjc', current, zonal_forward, preferred_element_type=...  16.8 us
    dot_general x8, matrix products, product(): jnp.einsum('mi,mio->mo', vectors, matrices, preferred_element_type=jnp.fl...  15.8 us
    dot_general x1, matrix products, per_device(): jnp.einsum('pq,nq->pn', readout_final, hidden, preferred_element_type=jnp...  12 us
  transfers between devices with their start and end apart: 2, of which 2 were waited for; matrix products, arithmetic and copies ran while one was open for 2% of the time, Pallas kernels for 0%

commit v1 on v0

--- a/solution.py
+++ b/solution.py
@@ -78,7 +78,9 @@
             partial_value, "space", scatter_dimension=0, tiled=True
         ).reshape(-1, 2, channels)
         mixed = mix_modes(spectrum.astype(jnp.bfloat16), spectral_weight[layer_index])
-        all_modes = lax.all_gather(mixed, "space", axis=0, tiled=True).reshape(KY, KX, 2, channels)
+        all_modes = jnp.concatenate(
+            lax.all_to_all(jnp.stack([mixed] * lax.axis_size("space")), "space", 0, 0), 0
+        ).reshape(KY, KX, 2, channels)
         returned = jnp.einsum(
             "hpqr,qkrc->hkpc", inverse_here, all_modes, preferred_element_type=jnp.float32
         )

time: 310 us -> 298 us (0.961)
  blocking collectives: 40.7 us -> 13.5 us
  waiting for transfers between devices: 106 us -> 117 us
  starting transfers between devices: 0.04 us -> 3.97 us
    all_gather x2 -> x0, blocking collectives: 40.7 us -> none  [per_device(): lax.all_gather(mixed, 'space', axis=0, tiled=True)]
    all_to_all x0 -> x1, blocking collectives: none -> 13.5 us  [per_device(): lax.all_to_all(jnp.stack([mixed] * lax.axis_size('space')), 'space', 0, 0)]
    all_to_all x0 -> x1, waiting for transfers between devices: none -> 9.38 us  [per_device(): lax.all_to_all(jnp.stack([mixed] * lax.axis_size('space')), 'space', 0, 0)]
    all_to_all x0 -> x1, starting transfers between devices: none -> 3.75 us  [per_device(): lax.all_to_all(jnp.stack([mixed] * lax.axis_size('space')), 'space', 0, 0)]
  transfers between devices with their start and end apart: 2 -> 3, of which waited for: 2 -> 3; matrix products, arithmetic and copies ran while one was open for 2% -> 2% of each run, Pallas kernels for 0% -> 0%
where the time goes in v1:
time: 298 us; the launch traced here: 297 us
  matrix products  117 us (39%)
  waiting for transfers between devices  117 us (39%)
  local copies, waits for them, and re-layouts  29.6 us (10%)
  between operations  13.6 us (5%)
  blocking collectives  13.5 us (5%)
  starting transfers between devices  3.97 us (1%)
    reduce_scatter x2, waiting for transfers between devices, per_device(): lax.psum_scatter(partial_value, 'space', scatter_dimension=0, tiled=True)  107 us
    dot_general x2, matrix products, per_device(): jnp.dot(current.reshape(-1, channels), local_weight[layer_index], preferr...  48.4 us
    dot_general x2, matrix products, per_device(): jnp.einsum('wj,hjc->hwc', zonal_inverse, returned, preferred_element_type...  22.8 us
    convert_element_type x1, local copies, waits for them, and re-layouts, per_device(): jax.nn.gelu(spread + pointwise + bias_now, approximate=True)  18.7 us
    dot_general x2, matrix products, per_device(): jnp.einsum('hwc,wj->hjc', current, zonal_forward, preferred_element_type=...  16.8 us
    dot_general x8, matrix products, product(): jnp.einsum('mi,mio->mo', vectors, matrices, preferred_element_type=jnp.fl...  15.8 us
    all_to_all x1, blocking collectives, per_device(): lax.all_to_all(jnp.stack([mixed] * lax.axis_size('space')), 'space', 0, 0)  13.5 us
    dot_general x1, matrix products, per_device(): jnp.einsum('pq,nq->pn', readout_final, hidden, preferred_element_type=jnp...  12 us
  transfers between devices with their start and end apart: 3, of which 3 were waited for; matrix products, arithmetic and copies ran while one was open for 2% of the time, Pallas kernels for 0%

profile of v1, /device:TPU:0, one launch (start us, length us, event | category | flops | bytes accessed | tf_op | source)
XLA Modules:
  0.0 297.3 jit_solution(11426819132431933586)
XLA Ops:
  6.5 0.0 copy-start
  6.5 0.0 copy-start.1
  6.5 0.0 reduce-scatter.3.cloned.1.call-start
  6.6 0.4 fusion.64
  7.0 0.1 fusion.101
  7.1 7.5 %convolution_convert_fusion.2 = bf16[32,24,256]{2,0,1:T(8,128)(2,1)S(1)} fusion(bf16[24,1152,256]{2,1,0:T(8,128)(2,1)} %param.6, f32[1152,16]{0,1:T(8,128)S(1)} %get-tuple-element.26, f32[1152,16]{0,1:T(8,128)S(1)} %get-tuple-element.25), kind=kOutput, calls=%fused_computation.49 | convolution fusion | flops 453292032 | bytes 14696448 | tf_op jit(solution)/shard_map/hwc,wj->hjc/dot_general | solution.py:69
  14.6 0.4 convolution_bitcast_fusion.3
  15.0 0.4 copy.63
  15.4 0.8 copy.119
  16.3 0.0 reduce-scatter.3.cloned.1.call-update
  16.3 0.0 copy-done.1
  16.3 0.1 fusion.110
  16.4 6.0 %slice_bitcast_fusion.1 = (bf16[16,2,256,256]{3,2,1,0:T(8,128)(2,1)}, bf16[16,2,256,256]{3,2,1,0:T(8,128)(2,1)}) fusion(bf16[2,16,2,256,256]{4,3,2,1,0:T(8,128)(2,1)} %param.7), kind=kLoop, calls=%fused_computation.33 | loop fusion | bytes 16777216 | tf_op jit(solution)/shard_map/squeeze | solution.py:80
  22.4 52.9 %reduce-scatter.3.cloned.1.call-done = f32[16,512]{1,0:T(8,128)} async-done(((f32[256,512]{1,0:T(8,128)}), f32[16,512]{1,0:T(8,128)}) %reduce-scatter.3.cloned.1.call-update) | async-done | bytes 32784 | tf_op jit(solution)/shard_map/reduce_scatter | solution.py:77
  75.3 0.8 convert_element_type.154
  76.1 2.0 fusion.29
  78.1 2.0 fusion.28
  80.1 2.0 fusion.27
  82.1 2.0 fusion.30
  84.1 0.9 stack.46
  85.0 3.7 %all-to-all-start = ((bf16[16,16,2,256]{3,2,1,0:T(2,128)(2,1)}), bf16[16,16,2,256]{3,2,1,0:T(2,128)(2,1)S(1)}, u32[]{:S(2)}, u32[]{:S(2)}) async-start(bf16[16,16,2,256]{3,2,1,0:T(2,128)(2,1)} %stack.46), calls=%async_computation.1 | async-start | bytes 524288 | tf_op jit(solution)/shard_map/all_to_all | solution.py:82
  88.8 0.2 reduce-scatter.5.cloned.1.call-start
  89.0 0.4 fusion.61
  89.4 9.4 %all-to-all-done = bf16[16,16,2,256]{3,2,1,0:T(2,128)(2,1)S(1)} async-done(((bf16[16,16,2,256]{3,2,1,0:T(2,128)(2,1)}), bf16[16,16,2,256]{3,2,1,0:T(2,128)(2,1)S(1)}, u32[]{:S(2)}, u32[]{:S(2)}) %all-to-all-start) | async-done | bytes 262176 | tf_op jit(solution)/shard_map/all_to_all | solution.py:82
  98.8 0.3 fusion.38
  99.1 0.0 copy-start.2
  99.1 11.4 %fusion.43 = f32[24,256,1152,1]{2,1,3,0:T(8,128)} fusion(bf16[24,16,2,256]{3,0,2,1:T(8,128)(2,1)S(1)} %fusion.38, f32[1152,16,1]{0,1,2:T(8,128)S(1)} %get-tuple-element.24, f32[1152,16,1]{0,1,2:T(8,128)S(1)} %get-tuple-element.23), kind=kOutput, calls=%fused_computation.60 | convolution fusion | flops 453095424 | bytes 28852224 | tf_op jit(solution)/shard_map/wj,hjc->hwc/dot_general | solution.py:88
  110.5 0.0 copy-done.2
  110.5 24.0 %fusion.7 = bf16[24,1152,256]{1,2,0:T(8,128)(2,1)} fusion(f32[24,256,1152,1]{2,1,3,0:T(8,128)} %fusion.43, bf16[24,1152,256]{2,1,0:T(8,128)(2,1)} %param.6, f32[256]{0:T(256)S(1)} %bitcast.208, bf16[2,256,256]{2,1,0:T(8,128)(2,1)S(1)} %copy-done.2), kind=kOutput, calls=%fused_computation.11 | convolution fusion | flops 3701735424 | bytes 56755200 | tf_op jit(solution)/shard_map/dot_general | solution.py:91
  134.5 9.2 %convolution_convert_fusion.1 = bf16[32,24,256]{2,0,1:T(8,128)(2,1)S(1)} fusion(bf16[24,1152,256]{1,2,0:T(8,128)(2,1)} %fusion.7, f32[1152,16]{0,1:T(8,128)S(1)} %get-tuple-element.26, f32[1152,16]{0,1:T(8,128)S(1)} %get-tuple-element.25), kind=kOutput, calls=%fused_computation.48 | convolution fusion | flops 453292032 | bytes 14696448 | tf_op jit(solution)/shard_map/hwc,wj->hjc/dot_general | solution.py:69
  143.8 0.4 convolution_bitcast_fusion.2
  144.1 0.4 copy.72
  144.5 0.8 copy.120
  145.4 0.0 reduce-scatter.5.cloned.1.call-update
  145.4 54.5 %reduce-scatter.5.cloned.1.call-done = f32[16,512]{1,0:T(8,128)} async-done(((f32[256,512]{1,0:T(8,128)}), f32[16,512]{1,0:T(8,128)}) %reduce-scatter.5.cloned.1.call-update) | async-done | bytes 32784 | tf_op jit(solution)/shard_map/reduce_scatter | solution.py:77
  199.9 0.8 convert_element_type.167
  200.7 2.0 fusion.31
  202.7 2.0 fusion.34
  204.7 2.0 fusion.33
  206.6 2.0 fusion.32
  208.7 0.2 stack.56
  208.9 13.5 %all_to_all.10 = bf16[16,16,2,256]{3,2,1,0:T(2,128)(2,1)S(1)} all-to-all(bf16[16,16,2,256]{3,2,1,0:T(2,128)(2,1)S(1)} %stack.56), channel_id=1, replica_groups=mesh['groups'=2,'space'=16] {'space'}, dimensions={0} | all-to-all | bytes 524288 | tf_op jit(solution)/shard_map/all_to_all | solution.py:82
  222.4 0.3 fusion.37
  222.7 11.4 %fusion.41 = f32[24,256,1152,1]{2,1,3,0:T(8,128)} fusion(bf16[24,16,2,256]{3,0,2,1:T(8,128)(2,1)S(1)} %fusion.37, f32[1152,16,1]{0,1,2:T(8,128)S(1)} %get-tuple-element.24, f32[1152,16,1]{0,1,2:T(8,128)S(1)} %get-tuple-element.23), kind=kOutput, calls=%fused_computation.58 | convolution fusion | flops 453095424 | bytes 28852224 | tf_op jit(solution)/shard_map/wj,hjc->hwc/dot_general | solution.py:88
  234.1 24.4 %fusion.15 = bf16[24,1152,256]{1,2,0:T(8,128)(2,1)} fusion(f32[24,256,1152,1]{2,1,3,0:T(8,128)} %fusion.41, bf16[24,1152,256]{1,2,0:T(8,128)(2,1)} %fusion.7, f32[256]{0:T(256)S(1)} %bitcast.207, bf16[2,256,256]{2,1,0:T(8,128)(2,1)S(1)} %copy-done.2), kind=kOutput, calls=%fused_computation.19 | convolution fusion | flops 3701735424 | bytes 56755200 | tf_op jit(solution)/shard_map/dot_general | solution.py:91
  258.6 0.0 copy-start.3
  258.6 18.7 %copy.80 = bf16[24,1152,256]{2,1,0:T(8,128)(2,1)} copy(bf16[24,1152,256]{1,2,0:T(8,128)(2,1)} %fusion.15) | data formatting | bytes 28311552 | tf_op jit(solution)/shard_map/convert_element_type | solution.py:98
  277.2 0.0 copy-done
  277.2 0.0 copy-done.3
  277.2 12.0 %convolution_convert_fusion = bf16[27648,20]{0,1:T(8,128)(2,1)S(1)} fusion(bf16[20,256]{1,0:T(8,128)(2,1)S(1)} %copy-done.3, bf16[27648,256]{1,0:T(8,128)(2,1)} %bitcast.192, bf16[256,256]{1,0:T(8,128)(2,1)S(1)} %copy-done), kind=kOutput, calls=%fused_computation.3 | convolution fusion | flops 3971248128 | bytes 15403008 | tf_op jit(solution)/shard_map/pq,nq->pn/dot_general | solution.py:103
  289.2 0.2 copy.121
  289.4 1.1 slice.64
  (21 shorter events, 0.2 us)
Async XLA Ops:
  6.5 270.7 %copy-start = (bf16[256,256]{1,0:T(8,128)(2,1)S(1)}, bf16[256,256]{1,0:T(8,128)(2,1)}, u32[]{:S(2)}) copy-start(bf16[256,256]{1,0:T(8,128)(2,1)} %param.10) | copy-start | bytes 393220
  6.5 9.8 %copy-start.1 = (bf16[2,256]{1,0:T(2,128)(2,1)S(1)}, bf16[2,256]{1,0:T(2,128)(2,1)}, u32[]{:S(2)}) copy-start(bf16[2,256]{1,0:T(2,128)(2,1)} %param.9) | copy-start | bytes 3076
  6.5 68.8 %reduce-scatter.3.cloned.1.call-start = ((), (), s32[]{:S(2)}) async-start(), calls=%async_computation.4 | async-start | bytes 557056 | tf_op jit(solution)/shard_map/reduce_scatter | solution.py:77
  85.0 13.8 %all-to-all-start = ((bf16[16,16,2,256]{3,2,1,0:T(2,128)(2,1)}), bf16[16,16,2,256]{3,2,1,0:T(2,128)(2,1)S(1)}, u32[]{:S(2)}, u32[]{:S(2)}) async-start(bf16[16,16,2,256]{3,2,1,0:T(2,128)(2,1)} %stack.46), calls=%async_computation.1 | async-start | bytes 524288 | tf_op jit(solution)/shard_map/all_to_all | solution.py:82
  88.8 111.1 %reduce-scatter.5.cloned.1.call-start = ((), (), s32[]{:S(2)}) async-start(), calls=%async_computation.5 | async-start | bytes 557056 | tf_op jit(solution)/shard_map/reduce_scatter | solution.py:77
  99.1 11.4 %copy-start.2 = (bf16[2,256,256]{2,1,0:T(8,128)(2,1)S(1)}, bf16[2,256,256]{2,1,0:T(8,128)(2,1)}, u32[]{:S(2)}) copy-start(bf16[2,256,256]{2,1,0:T(8,128)(2,1)} %param.8) | copy-start | bytes 786436
  258.6 18.7 %copy-start.3 = (bf16[20,256]{1,0:T(8,128)(2,1)S(1)}, bf16[20,256]{1,0:T(8,128)(2,1)}, u32[]{:S(2)}) copy-start(bf16[20,256]{1,0:T(8,128)(2,1)} %param.11) | copy-start | bytes 30724
Sparse Core Ops, SparseCore 0:
  16.4 58.8 reduce-scatter.2
  145.5 54.3 reduce-scatter.4
